TPU v7x, 32 devices: a whole 2x2x4 slice. The times are simulated.
32 devices in a mesh: groups: 2 (over y), ep: 4 (over z), tp: 2 (over x), dp: 2 (over core).
Axes of the slice: x: 2, y: 2, z: 4, core: 2. Of those that a mesh axis runs over, the one named last changes fastest.
Arguments:
- tokens: bfloat16 [256, 5120], P(('groups', 'ep', 'tp', 'dp')), parts along dimension 0, may hold values from -6 to 6
- route_weights: float32 [256, 8], P(('groups', 'ep', 'tp', 'dp')), parts along dimension 0, may hold values from 0.1 to 1
- expert_ids: int32 [256, 8], P(('groups', 'ep', 'tp', 'dp')), parts along dimension 0, may hold values from 0 to 31, all different within a row; in each aligned block of 8 rows (0 to 7, 8 to 15, ...) at most 4 rows name the same one
- gate_weight: bfloat16 [32, 5120, 1024], P('ep', None, ('tp', 'dp')), may hold values from -0.078125 to 0.078125
- up_weight: bfloat16 [32, 5120, 1024], P('ep', None, ('tp', 'dp')), may hold values from -0.078125 to 0.078125
- down_weight: bfloat16 [32, 1024, 5120], P('ep', None, ('tp', 'dp')), may hold values from -0.1875 to 0.1875
Outputs:
- combined: bfloat16 [256, 5120], P(('groups', 'ep', 'tp', 'dp')), parts along dimension 0
There are 2 independent parts, one for each index of `groups`. A program takes and returns all parts, laid end to end along the dimension named above; an argument that names none is the same for every part. Nothing has to cross between parts.
Inputs may be any that keep to these rules, and one draw needn't show every extreme that they name: `expert_ids`: each row names 8 different experts. Among the 8 rows of one device no expert is named more than 4 times, and in every draw some device's rows name some expert exactly 4 times.
All inputs are finite; a program needn't handle non-finite values.
Results may differ from a plain program's by a relative error of at most 0.0057.
Values may be sent and summed in bfloat16 or wider, within the bound.
No kernel may reach another device: no remote copies, remote signals or barrier semaphores. Data moves between devices by JAX's collectives and lax.ppermute only.
A program may use at most 128 MiB of HBM per device.

v0:
```python
import jax
import jax.numpy as jnp
from jax import lax
from jax.sharding import PartitionSpec as P

CAP = 4


def route_table(ids, experts, capacity):
    tok_count, top_count = ids.shape
    flat = ids.reshape(-1)
    onehot = (flat[:, None] == jnp.arange(experts, dtype=jnp.int32)[None, :]).astype(jnp.int32)
    slots = jnp.sum(onehot * jnp.cumsum(onehot, axis=0), axis=1) - 1
    place = flat * capacity + slots
    owner = jnp.arange(tok_count * top_count, dtype=jnp.int32) // top_count
    table = jnp.full((experts * capacity,), tok_count, jnp.int32).at[place].set(owner)
    return (place, table)


def per_device(tokens, route_weights, expert_ids, gate_weight, up_weight, down_weight):
    n_owner = lax.axis_size("ep")
    tok_count, top_count = expert_ids.shape
    exp_local = gate_weight.shape[0]
    experts = exp_local * n_owner
    width = tokens.shape[1]
    place, table = route_table(expert_ids, experts, CAP)
    sendbuf = jnp.take(tokens, table, axis=0, mode="fill", fill_value=0).reshape(
        experts, CAP, width
    )
    arrived = lax.all_to_all(sendbuf, "ep", split_axis=0, concat_axis=0, tiled=True)
    arrived = arrived.reshape(1, n_owner, exp_local, CAP, width)
    piece = lax.all_gather(arrived, ("tp", "dp"), axis=0, tiled=True)
    gate = jnp.einsum("gsecd,edf->gsecf", piece, gate_weight, preferred_element_type=jnp.float32)
    up = jnp.einsum("gsecd,edf->gsecf", piece, up_weight, preferred_element_type=jnp.float32)
    hidden = (jax.nn.silu(gate) * up).astype(jnp.bfloat16)
    partial_out = jnp.einsum(
        "gsecf,efd->gsecd",
        lax.all_gather(hidden, ("tp", "dp"), axis=4, tiled=True),
        down_weight,
        preferred_element_type=jnp.float32,
    )
    expert_out = partial_out.astype(jnp.bfloat16)
    mine = lax.all_to_all(expert_out, ("tp", "dp"), split_axis=0, concat_axis=4, tiled=True)
    mine = mine.reshape(n_owner * exp_local, CAP, width)
    returned = lax.all_to_all(mine, "ep", split_axis=0, concat_axis=0, tiled=True)
    picked = jnp.take(returned.reshape(experts * CAP, width), place, axis=0)
    picked = picked.reshape(tok_count, top_count, width).astype(jnp.float32)
    combined = jnp.sum(picked * route_weights[:, :, None], axis=1)
    return combined.astype(jnp.bfloat16)


def solution(mesh):
    return jax.shard_map(
        per_device,
        mesh=mesh,
        in_specs=(
            P(("groups", "ep", "tp", "dp"), None),
            P(("groups", "ep", "tp", "dp"), None),
            P(("groups", "ep", "tp", "dp"), None),
            P("ep", None, ("tp", "dp")),
            P("ep", None, ("tp", "dp")),
            P("ep", None, ("tp", "dp")),
        ),
        out_specs=P(("groups", "ep", "tp", "dp"), None),
        check_vma=False,
    )
```

profile of v0, /device:TPU:0, one launch (start us, length us, event | category | flops | bytes accessed | tf_op | source)
XLA Modules:
  0.0 212.0 jit_solution(12040743795864728024)
XLA Ops:
  6.5 0.8 reshape.76
  7.3 0.7 broadcast_multiply_fusion
  8.2 0.2 select_reduce_fusion
  8.5 0.8 scatter_custom_fusion
  9.3 1.3 gather_fusion
  10.6 0.5 gather.13
  11.3 0.7 broadcast_select_fusion
  11.9 37.5 %all_to_all.25 = bf16[32,4,5120]{2,1,0:T(4,128)(2,1)S(1)} all-to-all(bf16[32,4,5120]{2,1,0:T(4,128)(2,1)S(1)} %broadcast_select_fusion), channel_id=1, replica_groups=mesh['groups'=2,'ep'=4,'tp'=2,'dp'=2] {'ep'}, dimensions={0} | all-to-all | bytes 2621440 | tf_op jit(solution)/shard_map/all_to_all | solution.py:30
  49.4 1.7 copy.13
  51.1 0.2 all-gather.5.cloned.1.call-start
  51.3 39.5 %all-gather.3.cloned.1.call-done = bf16[4,4,8,4,5120]{4,3,1,0,2:T(4,128)(2,1)} async-done(((bf16[1,4,8,4,5120]{4,3,1,0,2:T(4,128)(2,1)}), bf16[4,4,8,4,5120]{4,3,1,0,2:T(4,128)(2,1)}) %all-gather.3.cloned.1.call-update) | async-done | bytes 5242896 | tf_op jit(solution)/shard_map/all_gather | solution.py:32
  90.8 13.1 %fusion.12 = f32[4,4,8,4,256]{4,3,1,0,2:T(4,128)S(1)} fusion(bf16[4,4,8,4,5120]{4,3,1,0,2:T(4,128)(2,1)} %all-gather.3.cloned.1.call-done, bf16[8,5120,256]{2,1,0:T(8,128)(2,1)} %param.9), kind=kOutput, calls=%fused_computation.13 | convolution fusion | flops 1342177280 | bytes 26738688 | tf_op jit(solution)/shard_map/gsecd,edf->gsecf/dot_general | solution.py:33
  103.9 12.2 %fusion.21 = bf16[4,4,8,4,256]{4,3,1,0,2:T(4,128)(2,1)} fusion(bf16[4,4,8,4,5120]{4,3,1,0,2:T(4,128)(2,1)S(1)} %copy-done.4, bf16[8,5120,256]{2,1,0:T(8,128)(2,1)} %param.10, f32[4,4,8,4,256]{4,3,1,0,2:T(4,128)S(1)} %fusion.12), kind=kOutput, calls=%fused_computation.16 | convolution fusion | flops 1342963712 | bytes 27000832 | tf_op jit(solution)/shard_map/gsecd,edf->gsecf/dot_general | solution.py:34
  116.1 17.0 %all-gather.5.cloned.1.call-done = bf16[4,4,8,4,1024]{4,3,1,0,2:T(4,128)(2,1)} async-done(((bf16[4,4,8,4,256]{4,3,1,0,2:T(4,128)(2,1)}), bf16[4,4,8,4,1024]{4,3,1,0,2:T(4,128)(2,1)}) %all-gather.5.cloned.1.call-update) | async-done | bytes 1048592 | tf_op jit(solution)/shard_map/all_gather | solution.py:38
  133.1 11.3 %fusion.9 = bf16[4,4,8,4,1280]{4,3,1,0,2:T(4,128)(2,1)S(1)} fusion(bf16[4,4,8,4,1024]{4,3,1,0,2:T(4,128)(2,1)} %all-gather.5.cloned.1.call-done, bf16[8,1024,1280]{2,1,0:T(8,128)(2,1)} %param.11), kind=kOutput, calls=%fused_computation.10 | convolution fusion | flops 1342832640 | bytes 23330816 | tf_op jit(solution)/shard_map/gsecf,efd->gsecd/dot_general | solution.py:36
  144.4 0.5 copy.14
  144.9 19.7 %all_to_all.26 = bf16[4,4,8,4,1280]{4,3,1,2,0:T(4,128)(2,1)S(1)} all-to-all(bf16[4,4,8,4,1280]{4,3,1,2,0:T(4,128)(2,1)S(1)} %copy.14), channel_id=1, replica_groups=mesh['groups'=2,'ep'=4,'tp'=2,'dp'=2] {'tp','dp'}, dimensions={0} | all-to-all | bytes 2621440 | tf_op jit(solution)/shard_map/all_to_all | solution.py:43
  164.6 1.0 copy.22
  165.6 1.4 reshape.108
  167.0 4.7 %all-to-all-start.2 = ((bf16[32,4,5120]{2,1,0:T(4,128)(2,1)}), bf16[32,4,5120]{2,1,0:T(4,128)(2,1)S(1)}, u32[]{:S(2)}, u32[]{:S(2)}) async-start(bf16[32,4,5120]{2,1,0:T(4,128)(2,1)} %reshape.108), calls=%async_computation.2 | async-start | bytes 2621440 | tf_op jit(solution)/shard_map/all_to_all | solution.py:45
  171.8 30.9 %all-to-all-done.2 = bf16[32,4,5120]{2,1,0:T(4,128)(2,1)S(1)} async-done(((bf16[32,4,5120]{2,1,0:T(4,128)(2,1)}), bf16[32,4,5120]{2,1,0:T(4,128)(2,1)S(1)}, u32[]{:S(2)}, u32[]{:S(2)}) %all-to-all-start.2) | async-done | bytes 1310752 | tf_op jit(solution)/shard_map/all_to_all | solution.py:45
  202.7 0.3 reshape.79
  203.0 0.9 gather_fusion.1
  204.0 1.2 multiply_reduce_fusion
  (26 shorter events, 0.5 us)
Async XLA Ops:
  6.5 2.8 %copy-start = (bf16[8,5120]{1,0:T(8,128)(2,1)S(1)}, bf16[8,5120]{1,0:T(8,128)(2,1)}, u32[]{:S(2)}) copy-start(bf16[8,5120]{1,0:T(8,128)(2,1)} %param.6) | copy-start | bytes 245764
  6.5 84.3 %all-gather.3.cloned.1.call-start = ((), (), s32[]{:S(2)}) async-start(), calls=%async_computation.3 | async-start | bytes 6553600 | tf_op jit(solution)/shard_map/all_gather | solution.py:32
  51.1 82.0 %all-gather.5.cloned.1.call-start = ((), (), s32[]{:S(2)}) async-start(), calls=%async_computation.4 | async-start | bytes 1310720 | tf_op jit(solution)/shard_map/all_gather | solution.py:38
  90.8 13.1 %copy-start.4 = (bf16[4,4,8,4,5120]{4,3,1,0,2:T(4,128)(2,1)S(1)}, bf16[4,4,8,4,5120]{4,3,1,0,2:T(4,128)(2,1)}, u32[]{:S(2)}) copy-start(bf16[4,4,8,4,5120]{4,3,1,0,2:T(4,128)(2,1)} %all-gather.3.cloned.1.call-done) | copy-start | bytes 15728644
  167.0 4.8 %copy-start.2 = (s32[8,8]{1,0:T(8,128)S(1)}, s32[8,8]{1,0:T(8,128)}, u32[]{:S(2)}) copy-start(s32[8,8]{1,0:T(8,128)} %param.8) | copy-start | bytes 772
  167.0 35.7 %all-to-all-start.2 = ((bf16[32,4,5120]{2,1,0:T(4,128)(2,1)}), bf16[32,4,5120]{2,1,0:T(4,128)(2,1)S(1)}, u32[]{:S(2)}, u32[]{:S(2)}) async-start(bf16[32,4,5120]{2,1,0:T(4,128)(2,1)} %reshape.108), calls=%async_computation.2 | async-start | bytes 2621440 | tf_op jit(solution)/shard_map/all_to_all | solution.py:45
  203.0 1.0 copy-start.3
  203.0 2.1 %copy-start.1 = (bf16[8,5120]{1,0:T(8,128)(2,1)S(1)}, bf16[8,5120]{1,0:T(8,128)(2,1)}, u32[]{:S(2)}) copy-start(bf16[8,5120]{1,0:T(8,128)(2,1)} %param.6) | copy-start | bytes 245764
Sparse Core Ops, SparseCore 0:
  51.2 39.5 all-gather.2
  116.2 16.8 all-gather.4
where the time goes:
time: 212 us
  waiting for transfers between devices  87.3 us (41%)
  blocking collectives  57.2 us (27%)
  matrix products  36.6 us (17%)
  between operations  13.6 us (6%)
  local copies, waits for them, and re-layouts  9.45 us (4%)
  starting transfers between devices  4.95 us (2%)
  other arithmetic  2.91 us (1%)
    all_gather x1, waiting for transfers between devices, per_device(): piece = lax.all_gather(arrived, ('tp', 'dp'), axis=0, tiled=True)  39.5 us
    all_to_all x1, blocking collectives, per_device(): lax.all_to_all(sendbuf, 'ep', split_axis=0, concat_axis=0, tiled=True)  37.5 us
    all_to_all x1, waiting for transfers between devices, per_device(): lax.all_to_all(mine, 'ep', split_axis=0, concat_axis=0, tiled=True)  30.9 us
    all_to_all x1, blocking collectives, per_device(): lax.all_to_all(expert_out, ('tp', 'dp'), split_axis=0, concat_axis=4, til...  19.7 us
    all_gather x1, waiting for transfers between devices, per_device(): lax.all_gather(hidden, ('tp', 'dp'), axis=4, tiled=True)  17 us
    dot_general x1, matrix products, per_device(): jnp.einsum('gsecd,edf->gsecf', piece, gate_weight, preferred_element_type...  13.1 us
    dot_general x1, matrix products, per_device(): jnp.einsum('gsecd,edf->gsecf', piece, up_weight, preferred_element_type=j...  12.2 us
    dot_general x1, matrix products, per_device(): jnp.einsum('gsecf,efd->gsecd', lax.all_gather(hidden, ('tp', 'dp'), axis=...  11.3 us
  transfers between devices with their start and end apart: 3, of which 3 were waited for; matrix products, arithmetic and copies ran while one was open for 0% of the time, Pallas kernels for 0%

commit v1 on v0

--- a/solution.py
+++ b/solution.py
@@ -4,6 +4,22 @@
 from jax.sharding import PartitionSpec as P
 
 CAP = 4
+
+
+def product_in_turn(x, axis, dim, product):
+    size, index, rows = (lax.axis_size(axis), lax.axis_index(axis), x.shape[dim])
+    right = [(i, (i + 1) % size) for i in range(size)]
+    downward = [(i, (i - 1) % size) for i in range(size)]
+    middle = size // 2
+    from_left = from_right = x
+    total = product(x, index * rows)
+    for lap in range(1, middle + 1):
+        from_left = lax.ppermute(from_left, axis, right)
+        if lap < size - middle:
+            from_right = lax.ppermute(from_right, axis, downward)
+            total = total + product(from_right, (index + lap) % size * rows)
+        total = total + product(from_left, (index - lap) % size * rows)
+    return total
 
 
 def route_table(ids, experts, capacity):
@@ -33,11 +49,16 @@
     gate = jnp.einsum("gsecd,edf->gsecf", piece, gate_weight, preferred_element_type=jnp.float32)
     up = jnp.einsum("gsecd,edf->gsecf", piece, up_weight, preferred_element_type=jnp.float32)
     hidden = (jax.nn.silu(gate) * up).astype(jnp.bfloat16)
-    partial_out = jnp.einsum(
-        "gsecf,efd->gsecd",
-        lax.all_gather(hidden, ("tp", "dp"), axis=4, tiled=True),
-        down_weight,
-        preferred_element_type=jnp.float32,
+    partial_out = product_in_turn(
+        hidden,
+        ("tp", "dp"),
+        4,
+        lambda part, offset: jnp.einsum(
+            "gsecf,efd->gsecd",
+            part,
+            lax.dynamic_slice_in_dim(down_weight, offset, part.shape[4], axis=1),
+            preferred_element_type=jnp.float32,
+        ),
     )
     expert_out = partial_out.astype(jnp.bfloat16)
     mine = lax.all_to_all(expert_out, ("tp", "dp"), split_axis=0, concat_axis=4, tiled=True)

time: 212 us -> 202 us (0.953)
  waiting for transfers between devices: 87.3 us -> 73.4 us
    all_gather x1 -> x0, waiting for transfers between devices: 17 us -> none  [per_device(): lax.all_gather(hidden, ('tp', 'dp'), axis=4, tiled=True)]
    ppermute x0 -> x3, waiting for transfers between devices: none -> 2.88 us  [the longest x2 2.87 us: product_in_turn(): from_left = lax.ppermute(from_left, axis, right)]
    dot_general x1 -> x4, matrix products: 11.3 us -> 13.9 us  [per_device(): jnp.einsum('gsecf,efd->gsecd', part, lax.dynamic_slice_in_dim(down_weight...]
  transfers between devices with their start and end apart: 3 -> 5, of which waited for: 3 -> 3; matrix products, arithmetic and copies ran while one was open for 0% -> 5% of each run, Pallas kernels for 0% -> 0%
where the time goes in v1:
time: 202 us
  waiting for transfers between devices  73.4 us (36%)
  blocking collectives  57.5 us (28%)
  matrix products  38.5 us (19%)
  between operations  13.7 us (7%)
  local copies, waits for them, and re-layouts  9.42 us (5%)
  starting transfers between devices  6.2 us (3%)
  other arithmetic  2.94 us (1%)
    all_gather x1, waiting for transfers between devices, per_device(): piece = lax.all_gather(arrived, ('tp', 'dp'), axis=0, tiled=True)  39.7 us
    all_to_all x1, blocking collectives, per_device(): lax.all_to_all(sendbuf, 'ep', split_axis=0, concat_axis=0, tiled=True)  37.5 us
    all_to_all x1, waiting for transfers between devices, per_device(): lax.all_to_all(mine, 'ep', split_axis=0, concat_axis=0, tiled=True)  30.9 us
    all_to_all x1, blocking collectives, per_device(): lax.all_to_all(expert_out, ('tp', 'dp'), split_axis=0, concat_axis=4, til...  20 us
    dot_general x4, matrix products, per_device(): jnp.einsum('gsecf,efd->gsecd', part, lax.dynamic_slice_in_dim(down_weight...  13.9 us
    dot_general x1, matrix products, per_device(): jnp.einsum('gsecd,edf->gsecf', piece, gate_weight, preferred_element_type...  13.1 us
    dot_general x1, matrix products, per_device(): jnp.einsum('gsecd,edf->gsecf', piece, up_weight, preferred_element_type=j...  11.5 us
    all_to_all x1, starting transfers between devices, per_device(): lax.all_to_all(mine, 'ep', split_axis=0, concat_axis=0, tiled=True)  4.39 us
  transfers between devices with their start and end apart: 5, of which 3 were waited for; matrix products, arithmetic and copies ran while one was open for 5% of the time, Pallas kernels for 0%

profile of v1, /device:TPU:0, one launch (start us, length us, event | category | flops | bytes accessed | tf_op | source)
XLA Modules:
  0.0 201.7 jit_solution(151588689759469222)
XLA Ops:
  6.5 0.7 broadcast_multiply_fusion
  7.3 0.8 reshape.76
  8.5 0.8 scatter_custom_fusion
  9.3 1.3 gather_fusion
  10.6 0.5 gather.13
  11.3 0.7 broadcast_select_fusion
  11.9 37.5 %all_to_all.25 = bf16[32,4,5120]{2,1,0:T(4,128)(2,1)S(1)} all-to-all(bf16[32,4,5120]{2,1,0:T(4,128)(2,1)S(1)} %broadcast_select_fusion), channel_id=1, replica_groups=mesh['groups'=2,'ep'=4,'tp'=2,'dp'=2] {'ep'}, dimensions={0} | all-to-all | bytes 2621440 | tf_op jit(solution)/shard_map/all_to_all | solution.py:46
  49.4 1.7 copy.13
  51.2 39.7 %all-gather.2.cloned.1.call-done = bf16[4,4,8,4,5120]{4,3,1,0,2:T(4,128)(2,1)} async-done(((bf16[1,4,8,4,5120]{4,3,1,0,2:T(4,128)(2,1)}), bf16[4,4,8,4,5120]{4,3,1,0,2:T(4,128)(2,1)}) %all-gather.2.cloned.1.call-update) | async-done | bytes 5242896 | tf_op jit(solution)/shard_map/all_gather | solution.py:48
  90.8 13.1 %fusion.31 = f32[4,4,8,4,256]{4,3,1,0,2:T(4,128)S(1)} fusion(bf16[4,4,8,4,5120]{4,3,1,0,2:T(4,128)(2,1)} %all-gather.2.cloned.1.call-done, bf16[8,5120,256]{2,1,0:T(8,128)(2,1)} %param.9), kind=kOutput, calls=%fused_computation.26 | convolution fusion | flops 1342177280 | bytes 26738688 | tf_op jit(solution)/shard_map/gsecd,edf->gsecf/dot_general | solution.py:49
  103.9 11.5 %fusion.40 = bf16[4,4,8,4,256]{4,3,1,0,2:T(4,128)(2,1)S(1)} fusion(bf16[4,4,8,4,5120]{4,3,1,0,2:T(4,128)(2,1)S(1)} %copy-done.4, bf16[8,5120,256]{2,1,0:T(8,128)(2,1)} %param.10, f32[4,4,8,4,256]{4,3,1,0,2:T(4,128)S(1)} %fusion.31), kind=kOutput, calls=%fused_computation.29 | convolution fusion | flops 1342963712 | bytes 27000832 | tf_op jit(solution)/shard_map/gsecd,edf->gsecf/dot_general | solution.py:50
  115.7 1.5 collective-permute-start
  117.2 3.3 %fusion.10 = f32[8,1280,4,4,4]{1,4,3,2,0:T(4,128)S(1)} fusion(bf16[4,4,8,4,256]{4,3,1,0,2:T(4,128)(2,1)S(1)} %fusion.40, bf16[8,1024,1280]{2,1,0:T(8,128)(2,1)} %param.11, s32[]{:T(128)S(6)} %select_n.65), kind=kOutput, calls=%fused_computation.13 | convolution fusion | flops 335544320 | bytes 8126468 | tf_op jit(solution)/shard_map/gsecf,efd->gsecd/dot_general | solution.py:56
  120.5 2.9 %collective-permute-done.1 = bf16[4,4,8,4,256]{4,3,1,0,2:T(4,128)(2,1)S(1)} collective-permute-done((bf16[4,4,8,4,256]{4,3,1,0,2:T(4,128)(2,1)S(1)}, bf16[4,4,8,4,256]{4,3,1,0,2:T(4,128)(2,1)S(1)}, u32[]{:S(2)}, u32[]{:S(2)}) %collective-permute-start.1) | collective-permute-done | bytes 262176 | tf_op jit(solution)/shard_map/ppermute | solution.py:17
  123.4 3.3 %fusion.6 = f32[8,1280,4,4,4]{1,4,3,2,0:T(4,128)S(1)} fusion(bf16[4,4,8,4,256]{4,3,1,0,2:T(4,128)(2,1)S(1)} %collective-permute-done.1, bf16[8,1024,1280]{2,1,0:T(8,128)(2,1)} %param.11, s32[]{:T(128)S(6)} %select_n.73), kind=kOutput, calls=%fused_computation.9 | convolution fusion | flops 335544320 | bytes 8126468 | tf_op jit(solution)/shard_map/gsecf,efd->gsecd/dot_general | solution.py:56
  126.8 3.8 %fusion.19 = f32[8,1280,4,4,4]{1,4,3,2,0:T(4,128)S(1)} fusion(f32[8,1280,4,4,4]{1,4,3,2,0:T(4,128)S(1)} %fusion.6, f32[8,1280,4,4,4]{1,4,3,2,0:T(4,128)S(1)} %fusion.10, bf16[4,4,8,4,256]{4,3,1,0,2:T(4,128)(2,1)S(1)} %collective-permute-done, bf16[8,1024,1280]{2,1,0:T(8,128)(2,1)} %param.11, s32[]{:T(128)S(6)} %select_n.71), kind=kOutput, calls=%fused_computation.20 | convolution fusion | flops 336855040 | bytes 13369348 | tf_op jit(solution)/shard_map/gsecf,efd->gsecd/dot_general | solution.py:56
  130.5 3.5 %fusion.28 = bf16[4,4,8,4,1280]{4,3,1,0,2:T(4,128)(2,1)S(1)} fusion(f32[8,1280,4,4,4]{1,4,3,2,0:T(4,128)S(1)} %fusion.19, bf16[4,4,8,4,256]{4,3,1,0,2:T(4,128)(2,1)S(1)} %collective-permute-done.2, bf16[8,1024,1280]{2,1,0:T(8,128)(2,1)} %param.11, s32[]{:T(128)S(6)} %select_n.75), kind=kOutput, calls=%fused_computation.23 | convolution fusion | flops 336855040 | bytes 9437188 | tf_op jit(solution)/shard_map/gsecf,efd->gsecd/dot_general | solution.py:56
  134.5 20.0 %all_to_all.26 = bf16[4,4,8,4,1280]{4,3,1,2,0:T(4,128)(2,1)S(1)} all-to-all(bf16[4,4,8,4,1280]{4,3,1,2,0:T(4,128)(2,1)S(1)} %copy.14), channel_id=1, replica_groups=mesh['groups'=2,'ep'=4,'tp'=2,'dp'=2] {'tp','dp'}, dimensions={0} | all-to-all | bytes 2621440 | tf_op jit(solution)/shard_map/all_to_all | solution.py:64
  154.6 1.0 copy.25
  155.6 1.4 reshape.111
  157.0 4.4 %all-to-all-start.2 = ((bf16[32,4,5120]{2,1,0:T(4,128)(2,1)}), bf16[32,4,5120]{2,1,0:T(4,128)(2,1)S(1)}, u32[]{:S(2)}, u32[]{:S(2)}) async-start(bf16[32,4,5120]{2,1,0:T(4,128)(2,1)} %reshape.111), calls=%async_computation.2 | async-start | bytes 2621440 | tf_op jit(solution)/shard_map/all_to_all | solution.py:66
  161.5 30.9 %all-to-all-done.2 = bf16[32,4,5120]{2,1,0:T(4,128)(2,1)S(1)} async-done(((bf16[32,4,5120]{2,1,0:T(4,128)(2,1)}), bf16[32,4,5120]{2,1,0:T(4,128)(2,1)S(1)}, u32[]{:S(2)}, u32[]{:S(2)}) %all-to-all-start.2) | async-done | bytes 1310752 | tf_op jit(solution)/shard_map/all_to_all | solution.py:66
  192.7 0.9 gather_fusion.1
  193.6 1.2 multiply_reduce_fusion
  (32 shorter events, 1.8 us)
Async XLA Ops:
  6.5 2.8 %copy-start = (bf16[8,5120]{1,0:T(8,128)(2,1)S(1)}, bf16[8,5120]{1,0:T(8,128)(2,1)}, u32[]{:S(2)}) copy-start(bf16[8,5120]{1,0:T(8,128)(2,1)} %param.6) | copy-start | bytes 245764
  6.5 84.3 %all-gather.2.cloned.1.call-start = ((), (), s32[]{:S(2)}) async-start(), calls=%async_computation.3 | async-start | bytes 6553600 | tf_op jit(solution)/shard_map/all_gather | solution.py:48
  90.8 13.1 %copy-start.4 = (bf16[4,4,8,4,5120]{4,3,1,0,2:T(4,128)(2,1)S(1)}, bf16[4,4,8,4,5120]{4,3,1,0,2:T(4,128)(2,1)}, u32[]{:S(2)}) copy-start(bf16[4,4,8,4,5120]{4,3,1,0,2:T(4,128)(2,1)} %all-gather.2.cloned.1.call-done) | copy-start | bytes 15728644
  115.4 8.0 %collective-permute-start.1 = (bf16[4,4,8,4,256]{4,3,1,0,2:T(4,128)(2,1)S(1)}, bf16[4,4,8,4,256]{4,3,1,0,2:T(4,128)(2,1)S(1)}, u32[]{:S(2)}, u32[]{:S(2)}) collective-permute-start(bf16[4,4,8,4,256]{4,3,1,0,2:T(4,128)(2,1)S(1)} %fusion.40), channel_id=1, source_target_pairs={{0,1},{1,2},{2,3},{3,0},{4,5},{5,6},{6,7},{7,4},{8,9},{9,10},{10,1... | collective-permute-start | bytes 786440 | tf_op jit(solution)/shard_map/ppermute | solution.py:17
  115.7 11.1 %collective-permute-start = (bf16[4,4,8,4,256]{4,3,1,0,2:T(4,128)(2,1)S(1)}, bf16[4,4,8,4,256]{4,3,1,0,2:T(4,128)(2,1)S(1)}, u32[]{:S(2)}, u32[]{:S(2)}) collective-permute-start(bf16[4,4,8,4,256]{4,3,1,0,2:T(4,128)(2,1)S(1)} %fusion.40), channel_id=1, source_target_pairs={{0,3},{1,0},{2,1},{3,2},{4,7},{5,4},{6,5},{7,6},{8,11},{9,8},{10,9... | collective-permute-start | bytes 786440 | tf_op jit(solution)/shard_map/ppermute | solution.py:19
  123.4 7.1 %collective-permute-start.2 = (bf16[4,4,8,4,256]{4,3,1,0,2:T(4,128)(2,1)S(1)}, bf16[4,4,8,4,256]{4,3,1,0,2:T(4,128)(2,1)S(1)}, u32[]{:S(2)}, u32[]{:S(2)}) collective-permute-start(bf16[4,4,8,4,256]{4,3,1,0,2:T(4,128)(2,1)S(1)} %collective-permute-done.1), channel_id=1, source_target_pairs={{0,1},{1,2},{2,3},{3,0},{4,5},{5,6},{6,7},{7,4},{8,9},{9,10},{10,1... | collective-permute-start | bytes 786440 | tf_op jit(solution)/shard_map/ppermute | solution.py:17
  155.6 5.9 %copy-start.2 = (s32[8,8]{1,0:T(8,128)S(1)}, s32[8,8]{1,0:T(8,128)}, u32[]{:S(2)}) copy-start(s32[8,8]{1,0:T(8,128)} %param.8) | copy-start | bytes 772
  157.0 35.4 %all-to-all-start.2 = ((bf16[32,4,5120]{2,1,0:T(4,128)(2,1)}), bf16[32,4,5120]{2,1,0:T(4,128)(2,1)S(1)}, u32[]{:S(2)}, u32[]{:S(2)}) async-start(bf16[32,4,5120]{2,1,0:T(4,128)(2,1)} %reshape.111), calls=%async_computation.2 | async-start | bytes 2621440 | tf_op jit(solution)/shard_map/all_to_all | solution.py:66
  192.4 2.5 %copy-start.1 = (bf16[8,5120]{1,0:T(8,128)(2,1)S(1)}, bf16[8,5120]{1,0:T(8,128)(2,1)}, u32[]{:S(2)}) copy-start(bf16[8,5120]{1,0:T(8,128)(2,1)} %param.6) | copy-start | bytes 245764
  192.7 0.9 copy-start.3
Sparse Core Ops, SparseCore 0:
  51.2 39.5 all-gather.1
